TPU v7x, 128 devices: a whole 4x4x4 slice. The times are simulated.
128 devices in a mesh: prompts: 1, model: 16 (over z, y), resp: 8 (over x, core).
Axes of the slice: x: 4, y: 4, z: 4, core: 2. Of those that a mesh axis runs over, the one named last changes fastest.
Arguments:
- x_prompt: bfloat16 [1024, 4096], P(('prompts', 'resp'))
- x_resp: bfloat16 [8, 1024, 4096], P(('prompts', 'resp'))
- targets: int32 [8, 1024], P(('prompts', 'resp'))
- resp_lens: int32 [8], P(('prompts', 'resp'))
- attn_gain: float32 [2, 4096], replicated
- w_query: bfloat16 [2, 4096, 32, 128], P(None, None, 'model')
- w_key: bfloat16 [2, 4096, 32, 128], P(None, None, 'model')
- w_value: bfloat16 [2, 4096, 32, 128], P(None, None, 'model')
- w_out: bfloat16 [2, 32, 128, 4096], P(None, 'model')
- mlp_gain: float32 [2, 4096], replicated
- w_gate: bfloat16 [2, 4096, 11008], P(None, None, 'model')
- w_up: bfloat16 [2, 4096, 11008], P(None, None, 'model')
- w_down: bfloat16 [2, 11008, 4096], P(None, 'model')
- final_gain: float32 [4096], replicated
- w_vocab: bfloat16 [4096, 32768], P(None, 'model')
Outputs:
- output: float32 [8, 1024], P(('prompts', 'resp'))
All inputs are finite; a program needn't handle non-finite values.
Results may differ from a plain program's by a relative error of at most 0.002451.
Values are sent between devices in bfloat16 or wider.
A program may use at most 1 GiB of HBM per device.

v0:
```python
import functools

import jax
import jax.numpy as jnp
from jax import lax
from jax.experimental import pallas as pl
from jax.experimental.pallas import tpu as pltpu
from jax.sharding import PartitionSpec as P

MESH = pl.DeviceIdType.MESH
F32 = jnp.float32
BF16 = jnp.bfloat16
EPS = 1e-6
LANES = 128
PAIR = 2
RING = 4
COLUMNS = PAIR * LANES
SHARDS = RING * RING
PEERS = 8
BOTH = range(PAIR)
VMEM_BYTES = 67_000_000
LATE_ROWS = 640
LOGITS = 512
CHUNKS = 4
VMEM = pl.BlockSpec(memory_space=pltpu.VMEM)
ANY = pl.BlockSpec(memory_space=pl.ANY)
DMA = pltpu.SemaphoreType.DMA
KINDS = range(RING * 3)
SUM_FAR, SUM_NEAR, SUM_RELAY, SUM2_FAR, SUM2_NEAR, SUM2_RELAY, TAKE_OWN, TAKE_REST, TAKE_RELAY, TAKE2_OWN, TAKE2_REST, TAKE2_RELAY = KINDS


def block_of(color, first, second):
    return RING * first + second if color else RING * second + first


def pair(index):
    return pl.ds(PAIR * index, PAIR)


class Torus:
    def __init__(self, refs, send_sem, recv_sem):
        self.refs = refs
        self.far, self.near, self.relayed, self.sums, self.relayed2, self.sums2, self.rows = refs
        self.send_sem, self.recv_sem = send_sem, recv_sem
        me = lax.axis_index("model")
        z, y = me // RING, me % RING
        self.place = ((y, z), (z, y))
        along_y = [z * RING + self.step(y, way) for way in (1, -1)]
        along_z = [self.step(z, way) * RING + y for way in (1, -1)]
        self.neighbors = ((along_y, along_z), (along_z, along_y))

    def step(self, place, by):
        return (place + by + RING) % RING

    def enter(self):
        sem = pltpu.get_barrier_semaphore()
        for ring in self.neighbors[0]:
            for device in ring:
                pl.semaphore_signal(sem, device_id={"model": device}, device_id_type=MESH)

    def all_here(self):
        pl.semaphore_wait(pltpu.get_barrier_semaphore(), RING)

    def ends(self, kind, c, q, d):
        (p, s), way, other = self.place[q], 1 - PAIR * d, 1 - d
        far, near, relayed, sums, relayed2, sums2, rows = (ref.at[c, q] for ref in self.refs)
        own = sums.at[0]
        back_s, back_p = self.step(s, -way), self.step(p, -way)
        return {
            SUM_FAR: lambda: (far.at[pair(d)], relayed.at[d], relayed.at[d]),
            SUM_NEAR: lambda: (near.at[d], sums.at[d, pair(other)], sums.at[d, pair(other)]),
            SUM_RELAY: lambda: (relayed.at[d], sums.at[d, pair(d)], sums.at[d, pair(d)]),
            SUM2_FAR: lambda: (own.at[self.step(s, PAIR), d], relayed2.at[d], relayed2.at[d]),
            SUM2_NEAR: lambda: (own.at[self.step(s, way), other], sums2.at[d, other], sums2.at[d, other]),
            SUM2_RELAY: lambda: (relayed2.at[d], sums2.at[d, d], sums2.at[d, d]),
            TAKE_OWN: lambda: (rows.at[p, s, d], rows.at[p, s, d], rows.at[p, back_s, d]),
            TAKE_REST: lambda: (rows.at[p, s, other], rows.at[p, s, other], rows.at[p, back_s, other]),
            TAKE_RELAY: lambda: (rows.at[p, back_s, d], rows.at[p, back_s, d], rows.at[p, self.step(s, PAIR), d]),
            TAKE2_OWN: lambda: (rows.at[p, pair(d)], rows.at[p, pair(d)], rows.at[back_p, pair(d)]),
            TAKE2_REST: lambda: (rows.at[p, pair(other)], rows.at[p, pair(other)], rows.at[back_p, pair(other)]),
            TAKE2_RELAY: lambda: (rows.at[back_p, pair(d)], rows.at[back_p, pair(d)], rows.at[self.step(p, PAIR), pair(d)]),
        }[kind]()

    def copy(self, kind, c, q, d, src, dst):
        second_ring = kind in (SUM2_FAR, SUM2_NEAR, SUM2_RELAY, TAKE_OWN, TAKE_REST, TAKE_RELAY)
        return pltpu.make_async_remote_copy(
            src_ref=src, dst_ref=dst, send_sem=self.send_sem.at[c, q, d, kind], recv_sem=self.recv_sem.at[c, q, d, kind],
            device_id={"model": self.neighbors[q][second_ring][d]}, device_id_type=MESH)

    def send(self, c, q, d, kind):
        src, dst, _ = self.ends(kind, c, q, d)
        self.copy(kind, c, q, d, src, dst).start()

    def sent(self, c, q, *kinds):
        for kind in kinds:
            for d in BOTH:
                src, dst, _ = self.ends(kind, c, q, d)
                self.copy(kind, c, q, d, src, dst).wait_send()

    def arrived(self, c, q, d, *kinds):
        for kind in kinds:
            _, _, here = self.ends(kind, c, q, d)
            self.copy(kind, c, q, d, here, here).wait_recv()


def halves_of(ref):
    return ref[:, :COLUMNS], ref[:, COLUMNS:]


def halves(value):
    return value[:, :LANES], value[:, LANES:]


def store_block(ref, value):
    for half, part in enumerate(halves(value)):
        ref[half] = part


def add_block(ref, value):
    for half, part in enumerate(halves(value)):
        ref[half] += part


class Gather:
    def __init__(self, net):
        self.net = net

    def begin_rows(self, c, q):
        for kind in (TAKE_OWN, TAKE_REST):
            for d in BOTH:
                self.net.send(c, q, d, kind)

    def relay_rows(self, c, q):
        for d in BOTH:
            self.net.arrived(c, q, d, TAKE_OWN)
            self.net.send(c, q, d, TAKE_RELAY)

    def take_second(self, c, q):
        for d in BOTH:
            self.net.arrived(c, q, d, TAKE_REST, TAKE_RELAY)
        for kind in (TAKE2_OWN, TAKE2_REST):
            for d in BOTH:
                self.net.send(c, q, d, kind)

    def relay_last(self, c, q):
        for d in BOTH:
            self.net.arrived(c, q, d, TAKE2_OWN)
            self.net.send(c, q, d, TAKE2_RELAY)

    def complete(self, c, q):
        for d in BOTH:
            self.net.arrived(c, q, d, TAKE2_REST, TAKE2_RELAY)
        self.net.sent(c, q, TAKE_OWN, TAKE_REST, TAKE_RELAY, TAKE2_OWN, TAKE2_REST, TAKE2_RELAY)

    def middle(self):
        return [self.relay_rows, self.take_second, self.relay_last]


class Sum(Gather):
    def __init__(self, net, lhs_of, w_ref, finish):
        self.net, self.lhs_of, self.w_ref, self.finish = net, lhs_of, w_ref, finish

    def product(self, lhs, color, first, second):
        start = pl.multiple_of(block_of(color, first, second) * COLUMNS, COLUMNS)
        return jnp.dot(lhs, self.w_ref[:, pl.ds(start, COLUMNS)], preferred_element_type=F32)

    def begin(self, c, q):
        net, p, lhs = self.net, self.net.place[q][0], self.lhs_of(c, q)
        for k in range(RING):
            store_block(net.far.at[c, q, k], self.product(lhs, q, net.step(p, PAIR), k))
        for d in BOTH:
            net.send(c, q, d, SUM_FAR)
        for d in BOTH:
            for k in BOTH:
                store_block(net.near.at[c, q, d, k], self.product(lhs, q, net.step(p, 1 - PAIR * d), PAIR * (1 - d) + k))
            net.send(c, q, d, SUM_NEAR)

    def relay_sum(self, c, q):
        net, p, lhs = self.net, self.net.place[q][0], self.lhs_of(c, q)
        for d in BOTH:
            net.arrived(c, q, d, SUM_FAR)
            for k in BOTH:
                add_block(net.relayed.at[c, q, d, k], self.product(lhs, q, net.step(p, 1 - PAIR * d), PAIR * d + k))
            net.send(c, q, d, SUM_RELAY)

    def begin_second(self, c, q):
        net, lhs = self.net, self.lhs_of(c, q)
        for d in BOTH:
            net.arrived(c, q, d, SUM_NEAR, SUM_RELAY)
        for k in range(RING):
            for half, part in enumerate(halves(self.product(lhs, q, net.place[q][0], k))):
                net.sums[c, q, 0, k, half] += net.sums[c, q, 1, k, half] + part
        for kind in (SUM2_FAR, SUM2_NEAR):
            for d in BOTH:
                net.send(c, q, d, kind)
        net.sent(c, q, SUM_FAR)

    def relay_second(self, c, q):
        net = self.net
        for d in BOTH:
            net.arrived(c, q, d, SUM2_FAR)
            net.relayed2[c, q, d] += net.sums[c, q, 0, net.step(net.place[q][1], 1 - PAIR * d), d]
            net.send(c, q, d, SUM2_RELAY)

    def finish_sum(self, c, q):
        net = self.net
        net.sent(c, q, SUM_NEAR, SUM_RELAY)
        for d in BOTH:
            net.arrived(c, q, d, SUM2_NEAR, SUM2_RELAY)
        for half in BOTH:
            self.finish(c, q, half, net.sums[c, q, 0, net.place[q][1], half] + net.sums2[c, q, 0, half] + net.sums2[c, q, 1, half])
        self.begin_rows(c, q)

    def relay_rows(self, c, q):
        self.net.sent(c, q, SUM2_FAR, SUM2_NEAR, SUM2_RELAY)
        super().relay_rows(c, q)

    def middle(self):
        return [self.relay_sum, self.begin_second, self.relay_second, self.finish_sum, *super().middle()]


def normed(net, c, q, gain_ref, layer):
    rows = net.rows.shape[-PAIR]
    tile = PAIR * 8 if rows % (PAIR * 8) == 0 else 8
    spots = [(first, second, half) for first in range(RING) for second in range(RING) for half in BOTH]

    @pl.loop(0, rows // tile)
    def _(i):
        span = pl.ds(pl.multiple_of(i * tile, tile), tile)
        acts = [net.rows[(c, q) + spot + (span,)].astype(F32) for spot in spots]
        squares = functools.reduce(jnp.add, [v * v for v in acts])
        inv = lax.rsqrt(jnp.sum(squares, axis=-1, keepdims=True) / (LANES * len(acts)) + EPS)
        for spot, v in zip(spots, acts):
            column = block_of(q, *spot[:PAIR]) * COLUMNS + spot[PAIR] * LANES
            net.rows[(c, q) + spot + (span,)] = (v * inv * gain_ref[pl.ds(layer, 1), pl.ds(column, LANES)]).astype(BF16)


def rows_of(net, c, q):
    parts = []
    for upper in range(RING):
        for lower in range(RING):
            first, second = (upper, lower) if q else (lower, upper)
            parts += [net.rows[c, q, first, second, half] for half in BOTH]
    return jnp.concatenate(parts, axis=1)


def times_transposed(lhs, rhs):
    return lax.dot_general(lhs, rhs, (((1,), (1,)), ((), ())), preferred_element_type=F32)


def late_plan(width, count):
    plan, start = [], 0
    for buffer in BOTH:
        for slot in range(width // count):
            size = min(LATE_ROWS, width - start)
            if size:
                plan.append((buffer, slot * count, start, size))
            start += size
    return plan, width - start


def rope(value, cos, sin):
    return jnp.concatenate([v * cos + pltpu.roll(v, LANES // PAIR, 1) * sin for v in halves(value)], axis=1)


def put_projected(product, cos_ref, sin_ref, out_ref, span):
    for k in range(3):
        value = product(k * COLUMNS, COLUMNS)
        if k < PAIR:
            value = rope(value, cos_ref[span], sin_ref[span])
        out_ref[span, pl.ds(k * COLUMNS, COLUMNS)] = value.astype(BF16)


def statistics(product, count, target):
    top = total = picked = None
    for k in range(count // LOGITS):
        logits = product(k * LOGITS, LOGITS)
        here = jnp.max(logits, axis=-1, keepdims=True)
        ids = lax.broadcasted_iota(jnp.int32, logits.shape, 1) + k * LOGITS
        found = jnp.sum(jnp.where(ids == target, logits, 0.0), axis=-1, keepdims=True)
        if k:
            both = jnp.maximum(top, here)
            total = total * jnp.exp(top - both) + jnp.sum(jnp.exp(logits - both), axis=-1, keepdims=True)
            top, picked = both, picked + found
        else:
            top, total, picked = here, jnp.sum(jnp.exp(logits - here), axis=-1, keepdims=True), found
    lane = lax.broadcasted_iota(jnp.int32, (target.shape[0], LANES), 1)
    return jnp.where(lane == 0, top, jnp.where(lane == 1, total, picked))


def mega_kernel(chunks, layer, last, gain_ref, next_gain_ref, ids_ref, dealt_ref, old_ref, *args):
    if last:
        side_refs, args = (), args
    else:
        side_refs, args = args[:3], args[3:]
    w_out_hbm, w_gate_hbm, w_up_hbm, w_down_hbm, *args = args
    late_hbm, out_ref, *args = args
    if not last:
        new_res_ref, *args = args
    (w_out, w_gate, w_up, w_down, late_rest, res, inner, middle, stats,
     far, near, relayed, sums, relayed2, sums2, rows, w_sem, late_sem, send_sem, recv_sem, ready_sem) = args
    loads = [pltpu.make_async_copy(src.at[layer], dst, w_sem.at[i]) for i, (src, dst) in enumerate(
        ((w_out_hbm, w_out), (w_gate_hbm, w_gate), (w_up_hbm, w_up), (w_down_hbm, w_down)))]
    for load in loads:
        load.start()
    width, count = late_hbm.shape
    plan, left = late_plan(width, count)
    late = [(late_hbm.at[pl.ds(start, size)], (w_gate, w_up)[buffer].at[pl.ds(0, size), pl.ds(lane, count)]) for buffer, lane, start, size in plan]
    if left:
        late.append((late_hbm.at[pl.ds(width - left, left)], late_rest))
    late_loads = [pltpu.make_async_copy(src, dst, late_sem.at[i]) for i, (src, dst) in enumerate(late)]
    net = Torus((far, near, relayed, sums, relayed2, sums2, rows), send_sem, recv_sem)
    net.enter()
    net.all_here()

    part = rows.shape[-PAIR]

    def span_of(c, q=0, parts=1):
        return pl.ds(pl.multiple_of((PAIR * c + q) * part, 16), parts * part)

    def after_prompt(c, q=0, parts=1):
        return pl.ds(pl.multiple_of((PAIR * c + q) * part + LANES * last, 16), parts * part)

    def picked(c, ref, prompt):
        ids = ids_ref[after_prompt(c, parts=PAIR), :1]
        chosen = (ids == lax.broadcasted_iota(jnp.int32, (PAIR * part, PEERS * LANES), 1)).astype(BF16)
        value = jnp.dot(chosen, ref[...], preferred_element_type=F32)
        if prompt is not None:
            row = lax.broadcasted_iota(jnp.int32, (PAIR * part, LANES), 0) + PAIR * part * c
            chosen = (row == lax.broadcasted_iota(jnp.int32, (PAIR * part, LANES), 1)).astype(BF16)
            value += jnp.dot(chosen, prompt, preferred_element_type=F32)
        return value.astype(BF16)

    def put(ref, value, place_of):
        for q in BOTH:
            for half, columns in enumerate(halves(value)):
                ref[place_of(q) + (half,)] = columns[q * part:(q + 1) * part]

    def begin(c):
        prompts = (None, None) if last else halves_of(side_refs[PAIR])
        put(rows, picked(c, dealt_ref, prompts[0]), lambda q: (c, q) + net.place[q])
        if not last:
            put(res, picked(c, old_ref, prompts[1]), lambda q: (c, q))
        for q in BOTH:
            first.begin_rows(c, q)

    def finish(c, q, half, total):
        value = (middle[c, q, half].astype(F32) + total).astype(BF16)
        if not last:
            new_res_ref[span_of(c, q), pl.ds(half * LANES, LANES)] = value
        rows[(c, q) + net.place[q] + (half,)] = value

    first = Gather(net)
    second = Sum(net, lambda c, q: inner[c, q], w_down, finish)

    def project_out(c):
        for q in BOTH:
            first.complete(c, q)
        total = jnp.dot(jnp.concatenate([rows_of(net, c, q) for q in BOTH], axis=0), w_out[...], preferred_element_type=F32)
        for q in BOTH:
            for half, columns in enumerate(halves(total)):
                old = old_ref[after_prompt(c, q), pl.ds(half * LANES, LANES)] if last else res[c, q, half]
                value = (old.astype(F32) + columns[q * part:(q + 1) * part]).astype(BF16)
                middle[c, q, half] = value
                rows[(c, q) + net.place[q] + (half,)] = value
        for ring in net.neighbors[0]:
            for device in ring:
                pl.semaphore_signal(ready_sem.at[c], device_id={"model": device}, device_id_type=MESH)

    def begin_again(c):
        pl.semaphore_wait(ready_sem.at[c], RING)
        for q in BOTH:
            first.begin_rows(c, q)

    def hidden_of(c, stage, gain, row):
        for q in BOTH:
            stage.complete(c, q)
            normed(net, c, q, gain, row)
        return jnp.concatenate([rows_of(net, c, q) for q in BOTH], axis=0)

    def mlp(c):
        hidden = hidden_of(c, first, gain_ref, layer)
        value = (jax.nn.silu(times_transposed(hidden, w_gate[...])) * times_transposed(hidden, w_up[...])).astype(BF16)
        inner[c] = value.reshape(inner.shape[1:])
        for q in BOTH:
            second.begin(c, q)

    def after(c):
        hidden = hidden_of(c, second, next_gain_ref, 0 if last else layer + 1)

        def product(lane, size):
            parts = [jnp.dot(hidden[:, start:start + rows_here], (w_gate, w_up)[buffer][pl.ds(0, rows_here), pl.ds(at + lane, size)], preferred_element_type=F32)
                     for buffer, at, start, rows_here in plan]
            if left:
                parts.append(jnp.dot(hidden[:, width - left:], late_rest[:, pl.ds(lane, size)], preferred_element_type=F32))
            return functools.reduce(jnp.add, parts)

        if last:
            stats[span_of(c, parts=PAIR)] = statistics(product, count, ids_ref[after_prompt(c, parts=PAIR), 1:PAIR])
        else:
            put_projected(product, *side_refs[:PAIR], out_ref, span_of(c, parts=PAIR))

    def on_both(step):
        def run(c):
            for q in BOTH:
                step(c, q)
        return run

    gather = [on_both(step) for step in first.middle()]
    steps = [begin, *gather, project_out, begin_again, *gather, mlp, *map(on_both, second.middle())]
    at_mlp = steps.index(mlp)
    steps += [None] * max(0, at_mlp + chunks - len(steps)) + [after]

    @pl.loop(0, len(steps) + chunks - 1)
    def _(slot):
        @pl.when(slot == steps.index(project_out))
        def _():
            for load in loads:
                load.wait()

        @pl.when(slot == len(steps) - 1)
        def _():
            for load in late_loads:
                load.wait()

        for k, step in reversed(list(enumerate(steps))):
            if step is None:
                continue

            @pl.when(slot >= k)
            def _():
                @pl.when(slot < k + chunks)
                def _():
                    step(slot - k)

        @pl.when(slot == at_mlp + chunks - 1)
        def _():
            for load in late_loads:
                load.start()

    if last:
        out_ref[...] = jnp.zeros_like(out_ref)
        for k in range(stats.shape[0] // LANES):
            turned = stats[pl.ds(k * LANES, LANES)].T
            for i in range(3):
                out_ref[i, pl.ds(k, 1)] = turned[i:i + 1]


def mega(gain, next_gain, ids, dealt, old, sides, w_out, w_gate_t, w_up_t, w_down, late, layer, collective_id):
    last = not sides
    chunks = CHUNKS
    total = ids.shape[0] - LANES * last
    _, hidden, width = w_gate_t.shape
    rows = total // (PAIR * chunks)
    per = (chunks, PAIR)
    tile = (rows, LANES)
    count = late.shape[1]
    _, left = late_plan(width, count)

    sem = DMA(per + (PAIR, len(KINDS)))
    out = jax.ShapeDtypeStruct((3, PEERS, LANES), F32) if last else (
        jax.ShapeDtypeStruct((total, count), BF16), jax.ShapeDtypeStruct((total, COLUMNS), BF16))
    return pl.pallas_call(
        functools.partial(mega_kernel, chunks, layer, last),
        out_shape=out,
        in_specs=[VMEM] * (5 + len(sides)) + [ANY] * 5,
        out_specs=VMEM if last else (VMEM, VMEM),
        scratch_shapes=[
            pltpu.VMEM((width, COLUMNS), BF16),
            *[pltpu.VMEM((hidden, width), BF16) for _ in range(3)],
            pltpu.VMEM((left or 8, count), BF16),
            pltpu.VMEM(per + (PAIR,) + (tile if not last else (8, LANES)), BF16),
            pltpu.VMEM(per + (rows, hidden), BF16),
            pltpu.VMEM(per + (PAIR,) + tile, BF16),
            pltpu.VMEM((total if last else 8, LANES), F32),
            pltpu.VMEM(per + (RING, PAIR) + tile, F32),
            pltpu.VMEM(per + (PAIR, PAIR, PAIR) + tile, F32),
            pltpu.VMEM(per + (PAIR, PAIR, PAIR) + tile, F32),
            pltpu.VMEM(per + (PAIR, RING, PAIR) + tile, F32),
            pltpu.VMEM(per + (PAIR,) + tile, F32),
            pltpu.VMEM(per + (PAIR, PAIR) + tile, F32),
            pltpu.VMEM(per + (RING, RING, PAIR) + tile, BF16),
            DMA((RING,)), DMA((SHARDS,)), sem, sem, pltpu.SemaphoreType.REGULAR((chunks,)),
        ],
        compiler_params=pltpu.CompilerParams(collective_id=collective_id, has_side_effects=True, vmem_limit_bytes=VMEM_BYTES),
        name=f"mega{collective_id}",
    )(gain, next_gain, ids, dealt, old, *sides, w_out, w_gate_t, w_up_t, w_down, late)


TILE = 128
Q_TILE = 256
LOG2E = 1.4426950408889634
HELD = pltpu.VMEM((PEERS, PAIR, TILE, COLUMNS), BF16)
GATHER_SEMS = [DMA((PAIR, 3)), DMA((PAIR, 3)), DMA((RING,)), DMA((RING,))]


class Exchange:
    def __init__(self):
        self.me = lax.axis_index("resp")
        self.others = [(self.me + k) % PEERS for k in range(1, PEERS)]

    def enter(self, models=()):
        sem = pltpu.get_barrier_semaphore()
        for axis, devices in (("resp", self.others), ("model", models)):
            for device in devices:
                pl.semaphore_signal(sem, device_id={axis: device}, device_id_type=MESH)

    def all_here(self, models=()):
        pl.semaphore_wait(pltpu.get_barrier_semaphore(), len(self.others) + len(models))

    def copy(self, src, dst, send_sem, recv_sem, device):
        return pltpu.make_async_remote_copy(src_ref=src, dst_ref=dst, send_sem=send_sem, recv_sem=recv_sem,
                                            device_id={"resp": device}, device_id_type=MESH)

    def scatter(self, src_of, dst, send_sem, recv_sem):
        for device in self.others:
            self.copy(src_of(device), dst, send_sem.at[device], recv_sem.at[self.me], device).start()

    def collected(self, dst_of, recv_sem):
        for device in self.others:
            self.copy(dst_of(device), dst_of(device), recv_sem.at[device], recv_sem.at[device], device).wait_recv()

    def sent(self, src_of, send_sem, recv_sem):
        for device in self.others:
            self.copy(src_of(device), src_of(device), send_sem.at[device], recv_sem.at[device], device).wait_send()


class Router:
    def __init__(self, net, tiles, src_of, dst_of, sems):
        self.net, self.tiles, self.src_of, self.dst_of = net, tiles, src_of, dst_of
        self.send_sem, self.recv_sem = sems

    def send(self, t):
        self.net.scatter(lambda d: self.src_of(t, d), self.dst_of(t, self.net.me), self.send_sem.at[t], self.recv_sem.at[t])

    def collect(self, t):
        self.net.collected(lambda d: self.dst_of(t, d), self.recv_sem.at[t])

    def finish(self):
        for t in range(self.tiles):
            self.net.sent(lambda d: self.src_of(t, d), self.send_sem.at[t], self.recv_sem.at[t])


class Slices:
    def __init__(self, w_hbm, held, send_sem, recv_sem):
        self.w, self.held, self.send_sem, self.recv_sem = w_hbm, held, send_sem, recv_sem
        self.me, home = lax.axis_index("model"), lax.axis_index("resp")
        self.homes = (home, (home + RING) % PEERS)
        self.others = [(self.me + k) % SHARDS for k in range(1, SHARDS)]

    def part(self, which, device):
        rows = pl.ds(pl.multiple_of(self.homes[which] * 32, 32), 32)
        return self.w.at[:, rows, pl.ds(pl.multiple_of(device * COLUMNS, COLUMNS), COLUMNS)]

    def own(self, which):
        return pltpu.make_async_copy(self.part(which, self.me), self.held.at[self.homes[which], :, self.me], self.send_sem.at[which, self.me])

    def copy(self, which, device, place):
        return pltpu.make_async_remote_copy(
            src_ref=self.part(which, device), dst_ref=self.held.at[self.homes[which], :, place], send_sem=self.send_sem.at[which, device],
            recv_sem=self.recv_sem.at[which, place], device_id={"model": device}, device_id_type=MESH)

    def start(self):
        for which in BOTH:
            self.own(which).start()
            for device in self.others:
                self.copy(which, device, self.me).start()

    def collect(self):
        for which in BOTH:
            for device in self.others:
                self.copy(which, device, device).wait_recv()
            self.own(which).wait()

    def finish(self):
        for which in BOTH:
            for device in self.others:
                self.copy(which, device, self.me).wait_send()


class RespGather:
    def __init__(self, net, held, ring_send, ring_recv, near_send, near_recv):
        self.net, self.held = net, held
        self.ring_sems, self.near_sems = (ring_send, ring_recv), (near_send, near_recv)
        x, core = net.me // PAIR, net.me % PAIR
        self.at = lambda by, here: (x + by + RING) % RING * PAIR + (core if here else 1 - core)

    def ring_copy(self, d, kind, ref):
        return self.net.copy(ref, ref, self.ring_sems[0].at[d, kind], self.ring_sems[1].at[d, kind], self.at(1 - PAIR * d, True))

    def near_copy(self, kind, ref):
        return self.net.copy(ref, ref, self.near_sems[0].at[kind], self.near_sems[1].at[kind], self.at(0, False))

    def sources(self, here):
        return [self.at(by, here) for by in (0, -1, 1, PAIR)]

    def start(self):
        for d in BOTH:
            self.ring_copy(d, 0, self.held.at[self.net.me, d]).start()
        self.near_copy(0, self.held.at[self.net.me]).start()

    def start_rest(self):
        for d in BOTH:
            self.ring_copy(d, 1, self.held.at[self.net.me, 1 - d]).start()

    def relay(self):
        for d in BOTH:
            ref = self.held.at[self.at(PAIR * d - 1, True), d]
            self.ring_copy(d, 0, ref).wait_recv()
            self.ring_copy(d, PAIR, ref).start()

    def share(self):
        for d in BOTH:
            device = self.at(PAIR * d - 1, True)
            self.ring_copy(d, 1, self.held.at[device, 1 - d]).wait_recv()
            self.near_copy(1 + d, self.held.at[device]).start()
        far = self.held.at[self.at(PAIR, True)]
        for d in BOTH:
            self.ring_copy(d, PAIR, far.at[d]).wait_recv()
        self.near_copy(3, far).start()

    def collect(self):
        for kind, device in enumerate(self.sources(False)):
            self.near_copy(kind, self.held.at[device]).wait_recv()

    def finish(self):
        for kind in range(3):
            for d in BOTH:
                self.ring_copy(d, kind, self.held.at[self.net.me, d]).wait_send()
        for kind in range(RING):
            self.near_copy(kind, self.held.at[self.net.me]).wait_send()


class ColumnGather(RespGather):
    def start(self):
        for d in BOTH:
            self.ring_copy(d, 0, self.held.at[self.net.me]).start()
        for kind, device in ((0, self.net.me), (3, self.at(PAIR, True))):
            self.near_copy(kind, self.held.at[device]).start()

    def share(self):
        for d in BOTH:
            ref = self.held.at[self.at(PAIR * d - 1, True)]
            self.ring_copy(d, 0, ref).wait_recv()
            self.near_copy(1 + d, ref).start()

    def finish(self):
        for d in BOTH:
            self.ring_copy(d, 0, self.held.at[self.net.me]).wait_send()
        for kind in range(RING):
            self.near_copy(kind, self.held.at[self.net.me]).wait_send()


def deal(rows):
    out = lax.broadcasted_iota(jnp.int32, (rows, rows), 0)
    src = lax.broadcasted_iota(jnp.int32, (rows, rows), 1)
    per = rows // PEERS
    return jnp.where(src == (out % per) * PEERS + out // per, 1.0, 0.0).astype(BF16)


def undeal(rows):
    out = lax.broadcasted_iota(jnp.int32, (rows, rows), 0)
    src = lax.broadcasted_iota(jnp.int32, (rows, rows), 1)
    per = rows // PEERS
    return jnp.where(src == (out % PEERS) * per + out // PEERS, 1.0, 0.0).astype(BF16)


def split_heads(raw_ref, w_ref):
    tile = PAIR * LANES
    out = lax.broadcasted_iota(jnp.int32, (tile, tile), 0)
    src = lax.broadcasted_iota(jnp.int32, (tile, tile), 1)
    pick = jnp.where(src == (out % LANES) * PAIR + out // LANES, 1.0, 0.0).astype(BF16)

    @pl.loop(0, raw_ref.shape[1] // (RING * tile))
    def _(b):
        raws = [raw_ref[i, pl.ds(pl.multiple_of((b * RING + k) * tile, tile), tile)] for k in range(RING) for i in range(3)]
        heads = jnp.dot(pick, jnp.concatenate(raws, axis=1), preferred_element_type=F32).astype(BF16)
        for k in range(RING):
            here = pl.ds(pl.multiple_of((b * RING + k) * LANES, LANES), LANES)
            for i in range(3):
                for h in BOTH:
                    at = (k * 3 + i) * LANES
                    w_ref[here, pl.ds(i * COLUMNS + h * LANES, LANES)] = heads[h * LANES:(h + 1) * LANES, at:at + LANES]


def norm_tile(x_ref, out_ref, gain_ref):
    for i in range(x_ref.shape[0] // 16):
        v = x_ref[pl.ds(16 * i, 16), :].astype(F32)
        inv = lax.rsqrt(jnp.mean(v * v, axis=-1, keepdims=True) + EPS)
        out_ref[pl.ds(16 * i, 16), :] = (v * inv * gain_ref[pl.ds(0, 1), :]).astype(BF16)


def softmax_mix(q, pieces):
    factor = LOG2E * 128 ** -0.5
    outs = []
    for h in range(2):
        lanes = slice(128 * h, 128 * h + 128)
        scores = []
        for keys, _, mask in pieces:
            s = lax.dot_general(q[:, lanes], keys[:, lanes], (((1,), (1,)), ((), ())), preferred_element_type=F32)
            scores.append(s if mask is None else jnp.where(mask, s, -jnp.inf))
        top = functools.reduce(jnp.maximum, [jnp.max(s, axis=-1, keepdims=True) for s in scores])
        probs = [jnp.exp2((s - top) * factor) for s in scores]
        total = functools.reduce(jnp.add, [jnp.sum(p, axis=-1, keepdims=True) for p in probs])
        mixed = functools.reduce(jnp.add, [jnp.dot(p.astype(BF16), values[:, lanes], preferred_element_type=F32) for p, (_, values, _) in zip(probs, pieces)])
        outs.append(mixed / total)
    return jnp.concatenate(outs, axis=1).astype(BF16)


def prompt_rows_of(held, which):
    return held[:, which].reshape(PEERS * TILE, COLUMNS)


def attend_response(t, q, held, k_own, v_own):
    row = lax.broadcasted_iota(jnp.int32, (Q_TILE, Q_TILE), 0)
    col = lax.broadcasted_iota(jnp.int32, (Q_TILE, Q_TILE), 1)
    pieces = [(prompt_rows_of(held, 0), prompt_rows_of(held, 1), None)]
    if t:
        pieces.append((k_own[:t * Q_TILE], v_own[:t * Q_TILE], None))
    span = slice(t * Q_TILE, (t + 1) * Q_TILE)
    pieces.append((k_own[span], v_own[span], col <= row))
    return softmax_mix(q, pieces)


def deal_mixed(router, t, mixed, stage, out):
    dealt = jnp.dot(deal(Q_TILE), mixed, preferred_element_type=F32).astype(BF16)
    stage[t] = dealt.reshape(PEERS, Q_TILE // PEERS, COLUMNS)
    router.send(t)
    out[router.net.me, t] = stage[t, router.net.me]


def first_attention_kernel(xp_hbm, xr_hbm, out_hbm, wq_hbm, wk_hbm, wv_hbm, gain_ref, cos_ref, sin_ref, info_ref,
                           mixed_out, res_out, info_out, prompt_out, next_hbm, columns_hbm,
                           xs, raw, w, even, odd, q_s, k_s, v_s, held, mixed_stage, res_stage,
                           x_sem, w_sem, ring_send, ring_recv, near_send, near_recv, info_send, info_recv, spread_held, spread_sem, *routes):
    net = Exchange()
    spread_sems, slice_sems, routes = routes[:RING], routes[RING:RING + PAIR], routes[RING + PAIR:]
    slices = Slices(out_hbm, spread_held, *slice_sems)
    columns = ColumnGather(net, spread_held, *spread_sems)
    mixed_router = Router(net, RING, lambda t, d: mixed_stage.at[t, d], lambda t, d: mixed_out.at[d, t], routes[:PAIR])
    res_router = Router(net, 1, lambda t, d: res_stage.at[d], lambda t, d: res_out.at[d], routes[PAIR:])
    prompt = RespGather(net, held, ring_send, ring_recv, near_send, near_recv)
    me = net.me
    column = pl.multiple_of(lax.axis_index("model") * COLUMNS, COLUMNS)

    def load(t):
        src = xp_hbm if isinstance(t, int) and t == 0 else xr_hbm.at[pl.ds(pl.multiple_of((t - 1) * TILE, TILE), TILE)]
        return pltpu.make_async_copy(src, xs.at[t], x_sem.at[t])

    load(0).start()
    weights, next_weights = ([pltpu.make_async_copy(src.at[layer], raw.at[i], w_sem.at[i]) for i, src in enumerate((wq_hbm, wk_hbm, wv_hbm))] for layer in BOTH)
    for copy in weights:
        copy.start()
    for t in range(1, 9):
        load(t).start()
    net.enter(slices.others)

    def project(t, hidden):
        span = pl.ds(pl.multiple_of(t * TILE, TILE), TILE)
        qkv = jnp.dot(hidden[...], w[...], preferred_element_type=F32)
        cos, sin = cos_ref[span], sin_ref[span]
        return span, rope(qkv[:, :COLUMNS], cos, sin).astype(BF16), rope(qkv[:, COLUMNS:512], cos, sin).astype(BF16), qkv[:, 512:].astype(BF16)

    load(0).wait()
    norm_tile(xs.at[0], even, gain_ref)
    for copy in weights:
        copy.wait()
    split_heads(raw, w)
    net.all_here(slices.others)
    slices.start()
    net.scatter(lambda d: info_ref.at[d], info_out.at[me], info_send, info_recv)
    info_out[me] = info_ref[me]
    for copy in next_weights:
        copy.start()
    load(1).wait()
    span, q, k, v = project(0, even)
    norm_tile(xs.at[1], odd, gain_ref)
    q_s[span] = q
    held[me, 0] = k
    held[me, 1] = v
    prompt.start()
    prompt.start_rest()
    for t in range(PAIR, 9):
        load(t).wait()
    spread = deal(TILE)

    @pl.loop(1, 9)
    def _(t):
        dealt = jnp.dot(spread, xs[t, :, pl.ds(column, COLUMNS)], preferred_element_type=F32).astype(BF16)
        res_stage[:, t - 1] = dealt.reshape(PEERS, TILE // PEERS, COLUMNS)

    res_out[me] = res_stage[me]

    def response_tile(t, here, there):
        span, q, k, v = project(t, here)
        norm_tile(xs.at[jnp.minimum(t + 1, 8)], there, gain_ref)
        q_s[span] = q
        own = pl.ds(pl.multiple_of((t - 1) * TILE, TILE), TILE)
        k_s[own] = k
        v_s[own] = v

    @pl.loop(0, RING)
    def _(i):
        response_tile(PAIR * i + 1, odd, even)
        response_tile(PAIR * i + PAIR, even, odd)

        @pl.when(i == 0)
        def _():
            prompt.relay()
            res_router.send(0)

        @pl.when(i == 1)
        def _():
            slices.collect()
            columns.start()

        pl.when(i == PAIR)(prompt.share)

    prompt.collect()
    for t in range(RING):
        mixed = attend_response(t, q_s[pl.ds(TILE + t * Q_TILE, Q_TILE)], held, k_s, v_s)
        deal_mixed(mixed_router, t, mixed, mixed_stage, mixed_out)
    columns.share()
    row = lax.broadcasted_iota(jnp.int32, (TILE, PEERS * TILE), 0) + me * TILE
    col = lax.broadcasted_iota(jnp.int32, (TILE, PEERS * TILE), 1)
    prompt_out[:, :COLUMNS] = softmax_mix(q_s[pl.ds(0, TILE)], [(prompt_rows_of(held, 0), prompt_rows_of(held, 1), col <= row)])
    prompt_out[:, COLUMNS:] = xs[0, :, pl.ds(column, COLUMNS)]
    for copy in next_weights:
        copy.wait()
    split_heads(raw, w)
    leave = pltpu.make_async_copy(w, next_hbm, w_sem.at[3])
    leave.start()
    columns.collect()
    out_copies = [pltpu.make_async_copy(spread_held.at[device, layer], columns_hbm.at[layer, :, device], spread_sem.at[layer, device])
                  for device in range(PEERS) for layer in BOTH]
    for copy in out_copies:
        copy.start()
    for router in (mixed_router, res_router):
        for t in range(router.tiles):
            router.collect(t)
        router.finish()
    net.collected(lambda d: info_out.at[d], info_recv)
    net.sent(lambda d: info_ref.at[d], info_send, info_recv)
    prompt.finish()
    columns.finish()
    slices.finish()
    leave.wait()
    for copy in out_copies:
        copy.wait()


def first_attention(x_prompt, x_resp, w_out, w_query, w_key, w_value, gain, cos, sin, info, collective_id):
    rows = TILE + x_resp.shape[0]
    width = x_resp.shape[1]
    return pl.pallas_call(
        first_attention_kernel,
        out_shape=(jax.ShapeDtypeStruct((PEERS, RING, 32, COLUMNS), BF16), jax.ShapeDtypeStruct((PEERS, 8, 16, COLUMNS), BF16),
                   jax.ShapeDtypeStruct((PEERS, 8, 128), jnp.int32), jax.ShapeDtypeStruct((TILE, PAIR * COLUMNS), BF16), jax.ShapeDtypeStruct((width, 3 * COLUMNS), BF16),
                   jax.ShapeDtypeStruct((PAIR, SHARDS, PEERS, 32, COLUMNS), BF16)),
        in_specs=[ANY] * 6 + [VMEM] * 4,
        out_specs=(VMEM,) * 4 + (ANY, ANY),
        scratch_shapes=[
            pltpu.VMEM((9, TILE, width), BF16), pltpu.VMEM((3, PAIR * width, LANES), BF16), pltpu.VMEM((width, 3 * COLUMNS), BF16), pltpu.VMEM((TILE, width), BF16), pltpu.VMEM((TILE, width), BF16),
            pltpu.VMEM((rows, COLUMNS), BF16), pltpu.VMEM((rows - TILE, COLUMNS), BF16), pltpu.VMEM((rows - TILE, COLUMNS), BF16),
            HELD, pltpu.VMEM((RING, PEERS, 32, COLUMNS), BF16), pltpu.VMEM((PEERS, 8, 16, COLUMNS), BF16),
            DMA((9,)), DMA((RING,)), *GATHER_SEMS, DMA((PEERS,)), DMA((PEERS,)),
            pltpu.VMEM((PEERS, PAIR, SHARDS, 32, COLUMNS), BF16), DMA((PAIR, PEERS)), *GATHER_SEMS, DMA((PAIR, SHARDS)), DMA((PAIR, SHARDS)),
            *[DMA((RING, PEERS)) for _ in BOTH], *[DMA((1, PEERS)) for _ in BOTH],
        ],
        compiler_params=pltpu.CompilerParams(collective_id=collective_id, has_side_effects=True, vmem_limit_bytes=VMEM_BYTES),
        name="first_attention",
    )(x_prompt, x_resp, w_out, w_query, w_key, w_value, gain, cos, sin, info)


def second_attention_kernel(qkv_ref, back_ref, mixed_out, stage, qkv_in, k_s, v_s, held, mixed_stage,
                            ring_send, ring_recv, near_send, near_recv, *routes):
    net = Exchange()
    me = net.me
    prompt = RespGather(net, held, ring_send, ring_recv, near_send, near_recv)
    router = Router(net, RING, lambda t, d: stage.at[t, d], lambda t, d: qkv_in.at[t, d], routes[:PAIR])
    mixed_router = Router(net, RING, lambda t, d: mixed_stage.at[t, d], lambda t, d: mixed_out.at[d, t], routes[PAIR:])
    for k in BOTH:
        held[me, k] = qkv_ref[pl.ds(0, TILE), pl.ds((k + 1) * COLUMNS, COLUMNS)]
    net.enter()
    count = back_ref.shape[1]

    def send_rows(t):
        place = lax.broadcasted_iota(jnp.int32, (Q_TILE, count), 0) + t * Q_TILE == back_ref[...]
        rows = jnp.dot(place.astype(BF16), qkv_ref[...], preferred_element_type=F32).astype(BF16)
        stage[t] = rows.reshape(PEERS, Q_TILE // PEERS, 3 * COLUMNS)
        if t == 0:
            net.all_here()
            prompt.start()
            prompt.start_rest()
        router.send(t)
        qkv_in[t, me] = stage[t, me]

    send_rows(0)
    prompt.relay()
    for t in range(1, RING):
        send_rows(t)
    prompt.share()
    prompt.collect()
    for t in range(RING):
        router.collect(t)
        rows = jnp.dot(undeal(Q_TILE), qkv_in[t].reshape(Q_TILE, 3 * COLUMNS), preferred_element_type=F32).astype(BF16)
        k_s[pl.ds(t * Q_TILE, Q_TILE)] = rows[:, COLUMNS:PAIR * COLUMNS]
        v_s[pl.ds(t * Q_TILE, Q_TILE)] = rows[:, PAIR * COLUMNS:]
        mixed = attend_response(t, rows[:, :COLUMNS], held, k_s, v_s)
        deal_mixed(mixed_router, t, mixed, mixed_stage, mixed_out)
    for t in range(RING):
        mixed_router.collect(t)
    for each in (router, mixed_router):
        each.finish()
    prompt.finish()


def second_attention(qkv, back, collective_id):
    rows = RING * Q_TILE
    wide = (32, 3 * COLUMNS)
    return pl.pallas_call(
        second_attention_kernel,
        out_shape=jax.ShapeDtypeStruct((PEERS, RING, 32, COLUMNS), BF16),
        in_specs=[VMEM, VMEM],
        out_specs=VMEM,
        scratch_shapes=[
            pltpu.VMEM((RING, PEERS) + wide, BF16), pltpu.VMEM((RING, PEERS) + wide, BF16),
            pltpu.VMEM((rows, COLUMNS), BF16), pltpu.VMEM((rows, COLUMNS), BF16),
            HELD, pltpu.VMEM((RING, PEERS, 32, COLUMNS), BF16), *GATHER_SEMS,
            *[DMA((RING, PEERS)) for _ in range(RING)],
        ],
        compiler_params=pltpu.CompilerParams(collective_id=collective_id, has_side_effects=True, vmem_limit_bytes=VMEM_BYTES),
        name=f"second_attention{collective_id}",
    )(qkv, back)


class Answer:
    def __init__(self, every, out_ref, stat_send, stat_recv, row_send, row_recv):
        self.every, self.out = every, out_ref
        self.stat_sems, self.row_sems = (stat_send, stat_recv), (row_send, row_recv)
        self.me, self.home = lax.axis_index("model"), lax.axis_index("resp")
        self.models = [(self.me + k) % SHARDS for k in range(1, SHARDS)]
        self.homes = [(self.home + k) % PEERS for k in range(1, PEERS)]

    def barrier(self):
        sem = pltpu.get_barrier_semaphore()
        for axis, devices in (("model", self.models), ("resp", self.homes)):
            for device in devices:
                pl.semaphore_signal(sem, device_id={axis: device}, device_id_type=MESH)
        pl.semaphore_wait(sem, len(self.models) + len(self.homes))

    def stat_copy(self, owner, device, place):
        ref = self.every.at[owner]
        return pltpu.make_async_remote_copy(
            src_ref=ref, dst_ref=ref, send_sem=self.stat_sems[0].at[device], recv_sem=self.stat_sems[1].at[place],
            device_id={"model": device}, device_id_type=MESH)

    def row_copy(self, owner, device, place):
        ref = self.out.at[owner]
        return pltpu.make_async_remote_copy(
            src_ref=ref, dst_ref=ref, send_sem=self.row_sems[0].at[device], recv_sem=self.row_sems[1].at[place],
            device_id={"resp": device}, device_id_type=MESH)

def combine_kernel(stats_ref, out_ref, every, *sems):
    net = Answer(every, out_ref, *sems)
    every[net.me] = stats_ref[...]
    net.barrier()
    for device in net.models:
        net.stat_copy(net.me, device, net.me).start()
    for device in net.models:
        net.stat_copy(device, device, device).wait_recv()
    shards = range(SHARDS)
    top = functools.reduce(jnp.maximum, [every[k, 0] for k in shards])
    total = functools.reduce(jnp.add, [every[k, 1] * jnp.exp(every[k, 0] - top) for k in shards])
    out_ref[net.home] = functools.reduce(jnp.add, [every[k, PAIR] for k in shards]) - top - jnp.log(total)
    for device in net.homes:
        net.row_copy(net.home, device, net.home).start()
    for device in net.homes:
        net.row_copy(device, device, device).wait_recv()
    for device in net.models:
        net.stat_copy(net.me, device, device).wait_send()
    for device in net.homes:
        net.row_copy(net.home, device, device).wait_send()


def combine(stats, collective_id):
    return pl.pallas_call(
        combine_kernel,
        out_shape=jax.ShapeDtypeStruct((PEERS, PEERS, LANES), F32),
        in_specs=[VMEM],
        out_specs=VMEM,
        scratch_shapes=[pltpu.VMEM((SHARDS,) + stats.shape, F32), *[DMA((SHARDS,)) for _ in BOTH], *[DMA((PEERS,)) for _ in BOTH]],
        compiler_params=pltpu.CompilerParams(collective_id=collective_id, has_side_effects=True),
        name="combine",
    )(stats)


ROPE_BASE = 10000.0
VARIANTS = (640, 768, 1024)


def rope_tables(positions):
    half = LANES // PAIR
    lane = jnp.arange(LANES)
    frequency = ROPE_BASE ** (-(lane % half).astype(F32) / half)
    angles = positions.astype(F32)[:, None] * frequency
    return jnp.cos(angles), jnp.sin(angles) * jnp.where(lane < half, -1.0, 1.0)


def solution(mesh):
    groups = mesh.shape['resp']
    row_axes = ('prompts', 'resp')
    head_spec = P(None, None, 'model', None)
    in_specs = (P(row_axes, None), P(row_axes, None, None), P(row_axes, None), P(row_axes), P(None, None), head_spec, head_spec, head_spec, P(None, 'model', None, None), P(None, None), P(None, None, 'model'), P(None, None, 'model'), P(None, 'model', None), P(None), P(None, 'model'))

    def device_step(x_prompt, x_resp, targets, resp_lens, attn_gain, w_query, w_key, w_value, w_out, mlp_gain, w_gate, w_up, w_down, final_gain, w_vocab):
        prompt_rows = x_prompt.shape[0]
        resp_len, width = x_resp.shape[1:]
        prompt_len = prompt_rows * groups
        me = lax.axis_index('model')
        home = lax.axis_index('resp')
        per = resp_len // groups
        gate_t, up_t = jnp.swapaxes(w_gate, 1, 2), jnp.swapaxes(w_up, 1, 2)
        out_flat = w_out.reshape(w_out.shape[0], COLUMNS, width)
        projections = [w.reshape(w.shape[0], PAIR * width, LANES) for w in (w_query, w_key, w_value)]
        prompt_pos = home * prompt_rows + jnp.arange(prompt_rows)

        cos, sin = rope_tables(jnp.concatenate([prompt_pos, prompt_len + jnp.arange(resp_len)]))
        info = jnp.concatenate([
            targets.reshape(per, groups).T[:, None, :],
            jnp.broadcast_to(resp_lens, (groups, groups - 1, per))], axis=1)
        mixed, res, infos, prompt, w_second, out_columns = first_attention(x_prompt, x_resp[0], out_flat, *projections, attn_gain, cos, sin, info, 0)
        lens = infos[:, 1, 0]
        need = (lens + groups - 1) // groups
        ends = jnp.sum(jnp.where(jnp.arange(groups)[:, None] >= jnp.arange(groups), need, 0), axis=1)
        starts = ends - need
        dealt = groups * per

        def finish_with(size, ident):
            def run(operands):
                mixed, res, prompt = operands
                slot = jnp.arange(prompt_rows + size) - prompt_rows
                which = jnp.sum((slot[:, None] >= ends).astype(jnp.int32), axis=1)
                row = slot - jnp.sum(jnp.where(which[:, None] == jnp.arange(groups), starts, 0), axis=1)
                real = (slot >= 0) & (slot < ends[-1])
                source = jnp.where(real, which * per + row, -1)
                chosen = source[:, None] == jnp.arange(dealt)
                wanted = jnp.sum(jnp.where(chosen, infos[:, 0, :].reshape(dealt), 0), axis=1) - me * w_vocab.shape[1]
                ids = jnp.where(jnp.arange(LANES) == 0, source[:, None], wanted[:, None])
                tables = rope_tables(jnp.where(slot < 0, home * prompt_rows + slot + prompt_rows, prompt_len + groups * row + home))
                weights = (out_columns.reshape(PAIR, width, COLUMNS), gate_t, up_t, w_down)
                qkv, new_res = mega(
                    mlp_gain, attn_gain, ids, mixed.reshape(dealt, COLUMNS), res.reshape(dealt, COLUMNS),
                    [*tables, prompt], *weights, w_second, 0, ident)
                part = per // RING
                back = jnp.where(real, (row // part) * (groups * part) + which * part + row % part, -1)
                mixed = second_attention(qkv, back[None], ident + 1)
                return mega(mlp_gain, final_gain[None], ids, mixed.reshape(dealt, COLUMNS), new_res, [], *weights, w_vocab, 1, ident + PAIR)
            return run

        smallest = sorted(VARIANTS)
        fit = sum((ends[-1] > size).astype(jnp.int32) for size in smallest[:-1])
        index = sum(jnp.where(fit == smallest.index(size), i, 0) for i, size in enumerate(VARIANTS))
        stats = lax.switch(index, [finish_with(size, 3 + 3 * i) for i, size in enumerate(VARIANTS)], (mixed, res, prompt))
        found = combine(stats, 1).reshape(groups, dealt)
        start = jnp.sum(jnp.where(jnp.arange(groups) == home, starts, 0))
        mine = lax.dynamic_slice(jnp.pad(found, ((0, 0), (0, per))), (0, start), (groups, per))
        log_probs = mine.T.reshape(resp_len)
        log_probs = jnp.where(jnp.arange(resp_len) < resp_lens[0], log_probs, 0.0)
        return log_probs[None, :]

    return jax.shard_map(device_step, mesh=mesh, in_specs=in_specs, out_specs=P(row_axes, None), check_vma=False)
```

profile of v0, /device:TPU:1, one launch (start us, length us, event | category | flops | bytes accessed | tf_op | source)
XLA Modules:
  0.0 486.5 jit_solution(2683689913078056917)
XLA Ops:
  0.7 0.5 broadcast.898
  1.2 1.3 reduce.5
  2.6 0.1 reshape.603
  2.7 0.6 concatenate.11.info_ref
  3.3 3.2 fusion.33
  6.6 0.0 copy-start
  6.6 54.6 %first_attention.1 = (bf16[8,4,32,256]{3,2,1,0:T(8,128)(2,1)}, bf16[8,8,16,256]{3,2,1,0:T(8,128)(2,1)}, s32[8,8,128]{2,1,0:T(8,128)}, bf16[128,512]{1,0:T(8,128)...) custom-call(bf16[128,4096]{1,0:T(8,128)(2,1)} %xp_hbm.1, bf16[1024,4096]{1,0:T(8,128)(2,1)} %bitcast.50, ...), custom_call_target="tpu_custom_call" | custom-call | tf_op jit(solution)/shard_map/first_attention/pallas_call | solution.py:855
  61.1 1.0 add_reduce_fusion
  62.2 0.1 select_reduce_fusion.6
  62.3 0.6 slice.26
  64.2 0.6 fusion.39
  66.8 0.0 copy-done
  66.8 391.7 %conditional.1 = (f32[3,8,128]{2,1,0:T(8,128)}) conditional(s32[]{:T(128)} %bitcast.29, (f32[4096]{0:T(1024)}, s32[8]{0:T(128)S(1)}, s32[8]{0:T(128)S(1)}, s32[8,8,128]{2,1,0:T(8,128)}, s32[]{:T(128)}, /*index=5*/bf16[8,4,32,256]{3,2,1,0:T(8,128)(2,1)}, bf16[8,8,16,256]{3,2,1,0:T(8,128)(2,1)}, s32[]{:T(128)}, ...), branch_computations={%region_1.5_spmd, %region_5.9_spmd, %region_9.13_spmd} | conditional | flops 4088834 | bytes 1876348 | solution.py:1064
  66.8 0.6 slice.11
  67.4 0.8 slice.18
  68.2 0.1 convert_reduce_fusion
  68.3 0.1 select_reduce_fusion.1
  68.4 0.6 broadcast_multiply_fusion
  69.0 0.6 select_reduce_fusion
  69.6 1.2 and_select_fusion.2.back_ref
  70.9 1.0 broadcast_select_fusion.ids_ref
  71.9 3.1 fusion
  75.0 173.9 %mega3.1 = (bf16[768,768]{1,0:T(8,128)(2,1)}, bf16[768,256]{1,0:T(8,128)(2,1)}) custom-call(f32[2,4096]{1,0:T(2,128)S(1)} %get-tuple-element.110.gain_ref, f32[2,4096]{1,0:T(2,128)} %get-tuple-element.117.next_gain_ref, s32[768,128]{1,0:T(8,128)} %broadcast_select_fusion.ids_ref, bf16[1024,256]{1,0:T(8,128)(2,1)} %bitcast.51, bf16[1024,256]{1,0:T(8,128)(2,1)} %bitcast.54, ...), custom_call_target="tpu_custom_call" | custom-call | tf_op jit(solution)/shard_map/cond/branch_0_fun/mega3/pallas_call | solution.py:463
  248.9 46.6 %second_attention4.1 = bf16[8,4,32,256]{3,2,1,0:T(8,128)(2,1)} custom-call(bf16[768,768]{1,0:T(8,128)(2,1)} %get-tuple-element.127.qkv_ref, s32[1,768]{1,0:T(1,128)} %and_select_fusion.2.back_ref), custom_call_target="tpu_custom_call" | custom-call | tf_op jit(solution)/shard_map/cond/branch_0_fun/second_attention4/pallas_call | solution.py:921
  295.5 153.9 %mega5.1 = f32[3,8,128]{2,1,0:T(8,128)} custom-call(f32[2,4096]{1,0:T(2,128)S(1)} %get-tuple-element.110.gain_ref, f32[1,4096]{1,0:T(1,128)} %bitcast.65, s32[768,128]{1,0:T(8,128)} %broadcast_select_fusion.ids_ref, bf16[1024,256]{1,0:T(8,128)(2,1)} %bitcast.61, bf16[768,256]{1,0:T(8,128)(2,1)} %get-tuple-element.128.old_ref, ...), custom_call_target="tpu_custom_call" | custom-call | tf_op jit(solution)/shard_map/cond/branch_0_fun/mega5/pallas_call | solution.py:463
  458.5 26.0 %combine.1 = f32[8,8,128]{2,1,0:T(8,128)} custom-call(f32[3,8,128]{2,1,0:T(8,128)} %get-tuple-element.207.stats_ref), custom_call_target="tpu_custom_call" | custom-call | tf_op jit(solution)/shard_map/combine/pallas_call | solution.py:987
  484.5 1.0 copy.21
  485.5 0.1 reshape.605
  485.6 0.6 compare_select_fusion.12
  (11 shorter events, 0.1 us)
Async XLA Ops:
  6.6 60.2 %copy-start = (f32[2,4096]{1,0:T(2,128)S(1)}, f32[2,4096]{1,0:T(2,128)}, u32[]{:S(2)}) copy-start(f32[2,4096]{1,0:T(2,128)} %param.27) | copy-start | bytes 98308
where the time goes:
time: 492 us; the launch traced here: 486 us
  Pallas kernels  455 us (92%)
  other arithmetic  13.7 us (3%)
  loops' own time  9.12 us (2%)
    pallas_call x2, Pallas kernels, mega(): pl.pallas_call(functools.partial(mega_kernel, chunks, layer, last), out_s...  328 us
    pallas_call x1, Pallas kernels, first_attention(): pl.pallas_call(first_attention_kernel, out_shape=(jax.ShapeDtypeStruct((P...  54.6 us
    pallas_call x1, Pallas kernels, second_attention(): pl.pallas_call(second_attention_kernel, out_shape=jax.ShapeDtypeStruct((P...  46.6 us
    pallas_call x1, Pallas kernels, combine(): pl.pallas_call(combine_kernel, out_shape=jax.ShapeDtypeStruct((PEERS, PEE...  26 us

commit v1 on v0

--- a/solution.py
+++ b/solution.py
@@ -542,35 +542,39 @@
 
 
 class Slices:
-    def __init__(self, w_hbm, held, send_sem, recv_sem):
-        self.w, self.held, self.send_sem, self.recv_sem = w_hbm, held, send_sem, recv_sem
+    def __init__(self, w_hbm, held, stage, stage_sem, send_sem, recv_sem):
+        self.held, self.stage, self.send_sem, self.recv_sem = held, stage, send_sem, recv_sem
         self.me, home = lax.axis_index("model"), lax.axis_index("resp")
         self.homes = (home, (home + RING) % PEERS)
         self.others = [(self.me + k) % SHARDS for k in range(1, SHARDS)]
 
+        self.loads = [pltpu.make_async_copy(w_hbm.at[:, pl.ds(pl.multiple_of(at * 32, 32), 32)], stage.at[which], stage_sem.at[which])
+                      for which, at in enumerate(self.homes)]
+
     def part(self, which, device):
-        rows = pl.ds(pl.multiple_of(self.homes[which] * 32, 32), 32)
-        return self.w.at[:, rows, pl.ds(pl.multiple_of(device * COLUMNS, COLUMNS), COLUMNS)]
-
-    def own(self, which):
-        return pltpu.make_async_copy(self.part(which, self.me), self.held.at[self.homes[which], :, self.me], self.send_sem.at[which, self.me])
+        return self.stage.at[which, :, :, pl.ds(pl.multiple_of(device * COLUMNS, COLUMNS), COLUMNS)]
 
     def copy(self, which, device, place):
         return pltpu.make_async_remote_copy(
             src_ref=self.part(which, device), dst_ref=self.held.at[self.homes[which], :, place], send_sem=self.send_sem.at[which, device],
             recv_sem=self.recv_sem.at[which, place], device_id={"model": device}, device_id_type=MESH)
 
+    def load(self):
+        for load in self.loads:
+            load.start()
+
     def start(self):
         for which in BOTH:
-            self.own(which).start()
+            self.loads[which].wait()
             for device in self.others:
                 self.copy(which, device, self.me).start()
+        for which in BOTH:
+            self.held[self.homes[which], :, self.me] = self.part(which, self.me)[...]
 
     def collect(self):
         for which in BOTH:
             for device in self.others:
                 self.copy(which, device, device).wait_recv()
-            self.own(which).wait()
 
     def finish(self):
         for which in BOTH:
@@ -734,7 +738,7 @@
                            xs, raw, w, even, odd, q_s, k_s, v_s, held, mixed_stage, res_stage,
                            x_sem, w_sem, ring_send, ring_recv, near_send, near_recv, info_send, info_recv, spread_held, spread_sem, *routes):
     net = Exchange()
-    spread_sems, slice_sems, routes = routes[:RING], routes[RING:RING + PAIR], routes[RING + PAIR:]
+    spread_sems, slice_sems, routes = routes[:RING], routes[RING:PAIR * RING], routes[PAIR * RING:]
     slices = Slices(out_hbm, spread_held, *slice_sems)
     columns = ColumnGather(net, spread_held, *spread_sems)
     mixed_router = Router(net, RING, lambda t, d: mixed_stage.at[t, d], lambda t, d: mixed_out.at[d, t], routes[:PAIR])
@@ -747,6 +751,7 @@
         src = xp_hbm if isinstance(t, int) and t == 0 else xr_hbm.at[pl.ds(pl.multiple_of((t - 1) * TILE, TILE), TILE)]
         return pltpu.make_async_copy(src, xs.at[t], x_sem.at[t])
 
+    slices.load()
     load(0).start()
     weights, next_weights = ([pltpu.make_async_copy(src.at[layer], raw.at[i], w_sem.at[i]) for i, src in enumerate((wq_hbm, wk_hbm, wv_hbm))] for layer in BOTH)
     for copy in weights:
@@ -754,6 +759,10 @@
     for t in range(1, 9):
         load(t).start()
     net.enter(slices.others)
+    net.all_here(slices.others)
+    slices.start()
+    net.scatter(lambda d: info_ref.at[d], info_out.at[me], info_send, info_recv)
+    info_out[me] = info_ref[me]
 
     def project(t, hidden):
         span = pl.ds(pl.multiple_of(t * TILE, TILE), TILE)
@@ -766,10 +775,6 @@
     for copy in weights:
         copy.wait()
     split_heads(raw, w)
-    net.all_here(slices.others)
-    slices.start()
-    net.scatter(lambda d: info_ref.at[d], info_out.at[me], info_send, info_recv)
-    info_out[me] = info_ref[me]
     for copy in next_weights:
         copy.start()
     load(1).wait()
@@ -864,7 +869,8 @@
             pltpu.VMEM((rows, COLUMNS), BF16), pltpu.VMEM((rows - TILE, COLUMNS), BF16), pltpu.VMEM((rows - TILE, COLUMNS), BF16),
             HELD, pltpu.VMEM((RING, PEERS, 32, COLUMNS), BF16), pltpu.VMEM((PEERS, 8, 16, COLUMNS), BF16),
             DMA((9,)), DMA((RING,)), *GATHER_SEMS, DMA((PEERS,)), DMA((PEERS,)),
-            pltpu.VMEM((PEERS, PAIR, SHARDS, 32, COLUMNS), BF16), DMA((PAIR, PEERS)), *GATHER_SEMS, DMA((PAIR, SHARDS)), DMA((PAIR, SHARDS)),
+            pltpu.VMEM((PEERS, PAIR, SHARDS, 32, COLUMNS), BF16), DMA((PAIR, PEERS)), *GATHER_SEMS,
+            pltpu.VMEM((PAIR, PAIR, 32, width), BF16), DMA((PAIR,)), DMA((PAIR, SHARDS)), DMA((PAIR, SHARDS)),
             *[DMA((RING, PEERS)) for _ in BOTH], *[DMA((1, PEERS)) for _ in BOTH],
         ],
         compiler_params=pltpu.CompilerParams(collective_id=collective_id, has_side_effects=True, vmem_limit_bytes=VMEM_BYTES),

time: 492 us -> 488 us (level)
  no operation moved by 1% of the time
where the time goes in v1:
time: 488 us; the launch traced here: 483 us
  Pallas kernels  452 us (93%)
  other arithmetic  13.7 us (3%)
  loops' own time  9.12 us (2%)
    pallas_call x2, Pallas kernels, mega(): pl.pallas_call(functools.partial(mega_kernel, chunks, layer, last), out_s...  329 us
    pallas_call x1, Pallas kernels, first_attention(): pl.pallas_call(first_attention_kernel, out_shape=(jax.ShapeDtypeStruct((P...  50.8 us
    pallas_call x1, Pallas kernels, second_attention(): pl.pallas_call(second_attention_kernel, out_shape=jax.ShapeDtypeStruct((P...  46.7 us
    pallas_call x1, Pallas kernels, combine(): pl.pallas_call(combine_kernel, out_shape=jax.ShapeDtypeStruct((PEERS, PEE...  25.4 us

profile of v1, /device:TPU:1, one launch (start us, length us, event | category | flops | bytes accessed | tf_op | source)
XLA Modules:
  0.0 483.3 jit_solution(5170311974079303487)
XLA Ops:
  0.7 0.5 broadcast.898
  1.2 1.3 reduce.5
  2.6 0.1 reshape.603
  2.7 0.6 concatenate.11.info_ref
  3.3 3.2 fusion.33
  6.6 0.0 copy-start
  6.6 50.8 %first_attention.1 = (bf16[8,4,32,256]{3,2,1,0:T(8,128)(2,1)}, bf16[8,8,16,256]{3,2,1,0:T(8,128)(2,1)}, s32[8,8,128]{2,1,0:T(8,128)}, bf16[128,512]{1,0:T(8,128)...) custom-call(bf16[128,4096]{1,0:T(8,128)(2,1)} %xp_hbm.1, bf16[1024,4096]{1,0:T(8,128)(2,1)} %bitcast.50, ...), custom_call_target="tpu_custom_call" | custom-call | tf_op jit(solution)/shard_map/first_attention/pallas_call | solution.py:860
  57.3 1.0 add_reduce_fusion
  58.4 0.1 select_reduce_fusion.6
  58.5 0.6 slice.26
  60.4 0.6 fusion.39
  63.0 0.0 copy-done
  63.0 392.9 %conditional.1 = (f32[3,8,128]{2,1,0:T(8,128)}) conditional(s32[]{:T(128)} %bitcast.29, (f32[4096]{0:T(1024)}, s32[8]{0:T(128)S(1)}, s32[8]{0:T(128)S(1)}, s32[8,8,128]{2,1,0:T(8,128)}, s32[]{:T(128)}, /*index=5*/bf16[8,4,32,256]{3,2,1,0:T(8,128)(2,1)}, bf16[8,8,16,256]{3,2,1,0:T(8,128)(2,1)}, s32[]{:T(128)}, ...), branch_computations={%region_1.5_spmd, %region_5.9_spmd, %region_9.13_spmd} | conditional | flops 4088834 | bytes 1876348 | solution.py:1070
  63.0 0.6 slice.11
  63.6 0.8 slice.18
  64.4 0.1 convert_reduce_fusion
  64.5 0.1 select_reduce_fusion.1
  64.6 0.6 broadcast_multiply_fusion
  65.2 0.6 select_reduce_fusion
  65.8 1.2 and_select_fusion.2.back_ref
  67.1 1.0 broadcast_select_fusion.ids_ref
  68.1 3.1 fusion
  71.2 174.7 %mega3.1 = (bf16[768,768]{1,0:T(8,128)(2,1)}, bf16[768,256]{1,0:T(8,128)(2,1)}) custom-call(f32[2,4096]{1,0:T(2,128)S(1)} %get-tuple-element.110.gain_ref, f32[2,4096]{1,0:T(2,128)} %get-tuple-element.117.next_gain_ref, s32[768,128]{1,0:T(8,128)} %broadcast_select_fusion.ids_ref, bf16[1024,256]{1,0:T(8,128)(2,1)} %bitcast.51, bf16[1024,256]{1,0:T(8,128)(2,1)} %bitcast.54, ...), custom_call_target="tpu_custom_call" | custom-call | tf_op jit(solution)/shard_map/cond/branch_0_fun/mega3/pallas_call | solution.py:463
  245.9 46.7 %second_attention4.1 = bf16[8,4,32,256]{3,2,1,0:T(8,128)(2,1)} custom-call(bf16[768,768]{1,0:T(8,128)(2,1)} %get-tuple-element.127.qkv_ref, s32[1,768]{1,0:T(1,128)} %and_select_fusion.2.back_ref), custom_call_target="tpu_custom_call" | custom-call | tf_op jit(solution)/shard_map/cond/branch_0_fun/second_attention4/pallas_call | solution.py:927
  292.7 154.2 %mega5.1 = f32[3,8,128]{2,1,0:T(8,128)} custom-call(f32[2,4096]{1,0:T(2,128)S(1)} %get-tuple-element.110.gain_ref, f32[1,4096]{1,0:T(1,128)} %bitcast.65, s32[768,128]{1,0:T(8,128)} %broadcast_select_fusion.ids_ref, bf16[1024,256]{1,0:T(8,128)(2,1)} %bitcast.61, bf16[768,256]{1,0:T(8,128)(2,1)} %get-tuple-element.128.old_ref, ...), custom_call_target="tpu_custom_call" | custom-call | tf_op jit(solution)/shard_map/cond/branch_0_fun/mega5/pallas_call | solution.py:463
  455.9 25.4 %combine.1 = f32[8,8,128]{2,1,0:T(8,128)} custom-call(f32[3,8,128]{2,1,0:T(8,128)} %get-tuple-element.207.stats_ref), custom_call_target="tpu_custom_call" | custom-call | tf_op jit(solution)/shard_map/combine/pallas_call | solution.py:993
  481.3 1.0 copy.21
  482.3 0.1 reshape.605
  482.4 0.6 compare_select_fusion.12
  (11 shorter events, 0.1 us)
Async XLA Ops:
  6.6 56.4 %copy-start = (f32[2,4096]{1,0:T(2,128)S(1)}, f32[2,4096]{1,0:T(2,128)}, u32[]{:S(2)}) copy-start(f32[2,4096]{1,0:T(2,128)} %param.27) | copy-start | bytes 98308
